TPU v7x, 16 devices: a whole 2x2x2 slice. The times are simulated.
16 devices in a mesh: sys: 4 (over z, y), row: 4 (over x, core).
Axes of the slice: x: 2, y: 2, z: 2, core: 2. Of those that a mesh axis runs over, the one named last changes fastest.
Arguments:
- positions: bfloat16 [32768, 128], P(('sys', 'row')), parts along dimension 0
- charges: float32 [32768], P(('sys', 'row')), parts along dimension 0
Outputs:
- output 1: float32 [32768, 128], P(('sys', 'row')), parts along dimension 0
- output 2: float32 [4], P('sys'), parts along dimension 0
There are 4 independent parts. A program takes and returns all parts, laid end to end along the dimension named above; each array names one.
All inputs are finite; a program needn't handle non-finite values.
Results may differ from a plain program's by a relative error of at most 0.001.
Values are sent between devices in bfloat16 or wider.
A program may use at most 1 GiB of HBM per device.

v0:
```python
import jax
import jax.numpy as jnp
from jax import lax
from jax.sharding import PartitionSpec as P


def pair_weight(host_x, host_q, host_sq, vis_x, vis_q, vis_sq, ell_sq):
    cross_dot = lax.dot_general(host_x, vis_x, (((1,), (1,)), ((), ())), preferred_element_type=jnp.float32)
    sq_dist = jnp.maximum(host_sq[:, None] + vis_sq[None, :] - 2.0 * cross_dot, 0.0)
    return host_q[:, None] * vis_q[None, :] * jnp.exp(-sq_dist / (2.0 * ell_sq))


def pair_forces(weight, host_x, vis_x):
    weight_bf = weight.astype(jnp.bfloat16)
    host_force = jnp.sum(weight, axis=1)[:, None] * host_x - jnp.dot(weight_bf, vis_x, preferred_element_type=jnp.float32)
    vis_force = jnp.sum(weight, axis=0)[:, None] * vis_x - lax.dot_general(weight_bf, host_x, (((0,), (0,)), ((), ())), preferred_element_type=jnp.float32)
    return host_force, vis_force


def row_sq(block_x):
    return jnp.sum(jnp.square(block_x.astype(jnp.float32)), axis=1)


def solution(mesh):
    row_count = mesh.shape["row"]
    full_steps = (row_count - 1) // 2
    has_middle = row_count % 2 == 0
    travel = row_count // 2
    forward = [(source, (source + 1) % row_count) for source in range(row_count)]
    homeward = [(source, (source - travel) % row_count) for source in range(row_count)]

    def device_body(pos_loc, chg_loc):
        rows_dev, feat_width = pos_loc.shape
        ell_sq = float(feat_width)
        half_rows = rows_dev // 2
        sq_loc = row_sq(pos_loc)
        local_ids = jnp.arange(rows_dev)
        diag_w = pair_weight(pos_loc, chg_loc, sq_loc, pos_loc, chg_loc, sq_loc, ell_sq)
        diag_w = jnp.where(local_ids[:, None] == local_ids[None, :], 0.0, diag_w)
        own_force = jnp.sum(diag_w, axis=1)[:, None] * pos_loc - jnp.dot(diag_w.astype(jnp.bfloat16), pos_loc, preferred_element_type=jnp.float32)
        own_energy = 0.5 * jnp.sum(diag_w)

        def full_step(step_idx, loop_state):
            vis_x, vis_q, vis_acc, force_acc, energy_acc = loop_state
            vis_x = lax.ppermute(vis_x, "row", forward)
            vis_q = lax.ppermute(vis_q, "row", forward)
            vis_acc = lax.ppermute(vis_acc, "row", forward)
            weight = pair_weight(pos_loc, chg_loc, sq_loc, vis_x, vis_q, row_sq(vis_x), ell_sq)
            host_force, vis_force = pair_forces(weight, pos_loc, vis_x)
            return (vis_x, vis_q, vis_acc + vis_force, force_acc + host_force, energy_acc + jnp.sum(weight))

        loop_state = (pos_loc, chg_loc, jnp.zeros((rows_dev, feat_width), jnp.float32), own_force, own_energy)
        vis_x, vis_q, vis_acc, force_acc, energy_acc = lax.fori_loop(0, full_steps, full_step, loop_state)
        if has_middle:
            vis_x = lax.ppermute(vis_x, "row", forward)
            vis_q = lax.ppermute(vis_q, "row", forward)
            vis_acc = lax.ppermute(vis_acc, "row", forward)
            vis_sq = row_sq(vis_x)
            low_half = lax.axis_index("row") < travel
            part_x = jnp.where(low_half, pos_loc[:half_rows], vis_x[half_rows:])
            part_q = jnp.where(low_half, chg_loc[:half_rows], vis_q[half_rows:])
            part_sq = jnp.where(low_half, sq_loc[:half_rows], vis_sq[half_rows:])
            other_x = jnp.where(low_half, vis_x, pos_loc)
            other_q = jnp.where(low_half, vis_q, chg_loc)
            other_sq = jnp.where(low_half, vis_sq, sq_loc)
            weight = pair_weight(part_x, part_q, part_sq, other_x, other_q, other_sq, ell_sq)
            part_force, other_force = pair_forces(weight, part_x, other_x)
            zero_half = jnp.zeros((half_rows, feat_width), jnp.float32)
            head_fill = jnp.concatenate([part_force, zero_half], axis=0)
            tail_fill = jnp.concatenate([zero_half, part_force], axis=0)
            force_acc = force_acc + jnp.where(low_half, head_fill, other_force)
            vis_acc = vis_acc + jnp.where(low_half, other_force, tail_fill)
            energy_acc = energy_acc + jnp.sum(weight)
        home_acc = lax.ppermute(vis_acc, "row", homeward)
        energy = lax.psum(energy_acc, "row")
        return (force_acc + home_acc) / ell_sq, energy.reshape(1)

    return jax.shard_map(device_body, mesh=mesh, in_specs=(P(("sys", "row"), None), P(("sys", "row"))), out_specs=(P(("sys", "row"), None), P("sys")), check_vma=False)
```

profile of v0, /device:TPU:0, one launch (start us, length us, event | category | flops | bytes accessed | tf_op | source)
XLA Modules:
  0.0 79.8 jit_solution(17948877591693631928)
XLA Ops:
  0.6 0.8 collective-permute-start
  1.4 2.6 %collective-permute-start.1 = (bf16[2048,128]{1,0:T(8,128)(2,1)}, bf16[2048,128]{1,0:T(8,128)(2,1)S(1)}, u32[]{:S(2)}, u32[]{:S(2)}) collective-permute-start(bf16[2048,128]{1,0:T(8,128)(2,1)} %param.2), channel_id=1, source_target_pairs={{0,1},{1,2},{2,3},{3,0},{4,5},{5,6},{6,7},{7,4},{8,9},{9,10},{10,1... | collective-permute-start | bytes 1572872 | tf_op jit(solution)/shard_map/while/body/eval_jaxpr/ppermute | solution.py:45
  4.0 1.0 %broadcast_in_dim.13 = f32[2048,128]{1,0:T(8,128)} broadcast(f32[]{:T(128)} %constant.9.clone.1), dimensions={} | broadcast | bytes 1048580 | tf_op jit(solution)/shard_map/broadcast_in_dim | solution.py:52
  5.1 0.1 collective-permute-start.4
  5.1 1.4 %fusion.16 = f32[2048]{0:T(1024)S(1)} fusion(bf16[2048,128]{1,0:T(8,128)(2,1)} %param.2), kind=kLoop, calls=%fused_computation.23 | loop fusion | flops 784384 | bytes 532480 | tf_op jit(solution)/shard_map/reduce_sum | solution.py:21
  6.5 0.0 copy-start.2
  6.5 0.0 copy-start
  6.5 0.0 collective-permute-done
  6.5 0.1 collective-permute-start.2
  6.6 13.7 %fusion.23 = (f32[]{:T(128)}, f32[2048]{0:T(1024)S(1)}, bf16[2048,2048]{0,1:T(8,128)(2,1)}) fusion(bf16[2048,128]{1,0:T(8,128)(2,1)} %param.2, f32[2048]{0:T(1024)S(1)} %fusion.16, f32[2048]{0:T(1024)} %param.3), kind=kOutput, calls=%fused_computation.40 | convolution fusion | flops 1128265728 | bytes 8937476 | tf_op jit(solution)/shard_map/dot_general | solution.py:8
  20.9 0.7 collective-permute-done.2
  21.6 0.0 copy-done.2
  21.6 0.0 collective-permute-done.1
  21.6 0.3 fusion.13
  22.0 0.0 collective-permute-start.3
  22.1 0.0 copy-done
  22.1 9.4 %fusion.22 = (f32[]{:T(128)}, f32[2048]{0:T(1024)S(1)}, f32[2048]{0:T(1024)S(1)}, bf16[2048,2048]{0,1:T(8,128)(2,1)S(1)}) fusion(bf16[2048,128]{1,0:T(8,128)(2,1)S(1)} %copy-done, bf16[2048,128]{1,0:T(8,128)(2,1)S(1)} %collective-permute-done.1, f32[2048]{0:T(1024)S(1)} %fusion.13, f32[2048]{0:T(1024)S(1)} %fusion.16, f32[2048]{0:T(1024)S(1)} %collective-permute-done, ...), kind=kOutput, calls=%fused_computation.39 | convolution fusion | flops 1124069376 | bytes 9486340 | tf_op jit(solution)/shard_map/while/body/eval_jaxpr/dot_general | solution.py:8
  31.5 0.0 copy-start.1
  31.5 0.0 collective-permute-done.3
  31.5 0.3 multiply_reduce_fusion
  31.8 0.0 collective-permute-done.4
  31.8 2.4 %fusion.15 = f32[2048,128]{1,0:T(8,128)S(1)} fusion(f32[2048,128]{1,0:T(8,128)S(1)} %collective-permute-done.4, bf16[2048,128]{1,0:T(8,128)(2,1)S(1)} %collective-permute-done.1, f32[2048]{0:T(1024)S(1)} %get-tuple-element.21, bf16[2048,128]{1,0:T(8,128)(2,1)S(1)} %copy-done, bf16[2048,2048]{0,1:T(8,128)(2,1)S(1)} %get-tuple-element.37), kind=kOutput, calls=%fused_computation.22 | convolution fusion | flops 1074790400 | bytes 11542528 | tf_op jit(solution)/shard_map/while/body/eval_jaxpr/dot_general | solution.py:16
  34.3 2.4 %collective-permute-start.5 = (f32[2048,128]{1,0:T(8,128)S(1)}, f32[2048,128]{1,0:T(8,128)S(1)}, u32[]{:S(2)}, u32[]{:S(2)}) collective-permute-start(f32[2048,128]{1,0:T(8,128)S(1)} %fusion.15), channel_id=1, source_target_pairs={{0,1},{1,2},{2,3},{3,0},{4,5},{5,6},{6,7},{7,4},{8,9},{9,10},{10,1... | collective-permute-start | bytes 3145736 | tf_op jit(solution)/shard_map/ppermute | solution.py:57
  36.7 0.1 broadcast_select_fusion
  36.8 5.2 %fusion.24 = (f32[]{:T(128)}, f32[2048]{0:T(1024)S(1)}, f32[1024]{0:T(1024)S(1)}, bf16[1024,2048]{1,0:T(8,128)(2,1)S(1)}) fusion(bf16[1024,128]{1,0:T(8,128)(2,1)S(1)} %slice_select_fusion, bf16[2048,128]{1,0:T(8,128)(2,1)S(1)} %broadcast_select_fusion, f32[2048]{0:T(1024)S(1)} %broadcast_select_fusion.1, f32[1024]{0:T(1024)S(1)} %slice_select_fusion.1, ...), kind=kOutput, calls=%fused_computation.41 | convolution fusion | flops 562033664 | bytes 5017604 | tf_op jit(solution)/shard_map/dot_general | solution.py:8
  42.0 0.0 copy-done.1
  42.0 0.0 slice-start
  42.0 1.3 %fusion.9 = f32[2048,128]{1,0:T(8,128)S(1)} fusion(bf16[1024,128]{1,0:T(8,128)(2,1)S(1)} %slice_select_fusion, bf16[1024,2048]{1,0:T(8,128)(2,1)S(1)} %get-tuple-element.38), kind=kOutput, calls=%fused_computation.11 | convolution fusion | flops 536870912 | bytes 5505024 | tf_op jit(solution)/shard_map/dot_general | solution.py:16
  43.4 0.0 slice-start.1
  43.4 1.3 %multiply_subtract_fusion.1 = f32[1024,128]{1,0:T(8,128)S(1)} fusion(bf16[1024,128]{1,0:T(8,128)(2,1)S(1)} %slice_select_fusion, f32[1024]{0:T(1024)S(1)} %get-tuple-element.36, bf16[2048,128]{1,0:T(8,128)(2,1)S(1)} %broadcast_select_fusion, bf16[1024,2048]{1,0:T(8,128)(2,1)S(1)} %get-tuple-element.38), kind=kOutput, calls=%fused_computation.32 | convolution fusion | flops 537264128 | bytes 5509120 | tf_op jit(solution)/shard_map/dot_general | solution.py:15
  44.6 3.9 %collective-permute-done.5 = f32[2048,128]{1,0:T(8,128)S(1)} collective-permute-done((f32[2048,128]{1,0:T(8,128)S(1)}, f32[2048,128]{1,0:T(8,128)S(1)}, u32[]{:S(2)}, u32[]{:S(2)}) %collective-permute-start.5) | collective-permute-done | bytes 1048608 | tf_op jit(solution)/shard_map/ppermute | solution.py:57
  48.6 1.3 %select_add_fusion = f32[2048,128]{1,0:T(8,128)} fusion(f32[2048,128]{1,0:T(8,128)S(1)} %collective-permute-done.5, f32[1024,128]{1,0:T(8,128)S(1)} %multiply_subtract_fusion.1, f32[2048,128]{1,0:T(8,128)S(1)} %fusion.9, bf16[2048,128]{1,0:T(8,128)(2,1)S(1)} %broadcast_select_fusion, f32[2048]{0:T(1024)S(1)} %get-tuple-element.26, pred[]{:T(512)S(6)} %lt.4), kind=kLoop, calls=%fused_computation.29 | loop fusion | flops 1310720 | bytes 4202497 | tf_op jit(solution)/shard_map/add | solution.py:72
  49.9 2.3 %collective-permute-start.6 = (f32[2048,128]{1,0:T(8,128)}, f32[2048,128]{1,0:T(8,128)}, u32[]{:S(2)}, u32[]{:S(2)}) collective-permute-start(f32[2048,128]{1,0:T(8,128)} %select_add_fusion), channel_id=1, source_target_pairs={{0,2},{1,3},{2,0},{3,1},{4,6},{5,7},{6,4},{7,5},{8,10},{9,11},{10,... | collective-permute-start | bytes 3145736 | tf_op jit(solution)/shard_map/ppermute | solution.py:74
  52.2 0.0 slice-done
  52.2 0.0 slice-done.1
  52.2 3.7 %fusion.6 = f32[2048,128]{1,0:T(8,128)} fusion(bf16[2048,128]{1,0:T(8,128)(2,1)S(1)} %copy-done, bf16[2048,2048]{0,1:T(8,128)(2,1)S(1)} %bitcast.18, f32[2048]{0:T(1024)S(1)} %get-tuple-element.24), kind=kOutput, calls=%fused_computation.10 | convolution fusion | flops 1074528256 | bytes 9969664 | tf_op jit(solution)/shard_map/dot_general | solution.py:40
  56.6 6.7 %fusion.4 = f32[2048,128]{1,0:T(8,128)} fusion(bf16[2048,128]{1,0:T(8,128)(2,1)S(1)} %collective-permute-done.1, bf16[2048,2048]{0,1:T(8,128)(2,1)} %copy-done.1), kind=kOutput, calls=%fused_computation.8 | convolution fusion | flops 1073741824 | bytes 9961472 | tf_op jit(solution)/shard_map/while/body/eval_jaxpr/dot_general | solution.py:15
  63.9 12.9 %psum.7 = f32[1]{0:T(128)} all-reduce(f32[1]{0:T(128)} %bitcast), channel_id=1, replica_groups=mesh['sys'=4,'row'=4] {'row'}, use_global_device_ids=true, to_apply=%region_11.12 | all-reduce | flops 1 | bytes 8 | tf_op jit(solution)/shard_map/psum | solution.py:75
  76.9 0.0 collective-permute-done.6
  76.9 3.0 %fusion.21 = f32[2048,128]{1,0:T(8,128)} fusion(f32[2048,128]{1,0:T(8,128)} %collective-permute-done.6, f32[2048,128]{1,0:T(8,128)} %fusion.6, f32[2048,128]{1,0:T(8,128)} %fusion.4, bf16[2048,128]{1,0:T(8,128)(2,1)S(1)} %copy-done, f32[1024,128]{1,0:T(8,128)S(1)} %multiply_subtract_fusion.1, f32[2048,128]{1,0:T(8,128)S(1)} %fusion.9, ...), kind=kLoop, calls=%fused_computation.28 | loop fusion | flops 2883584 | bytes 6832129 | tf_op jit(solution)/shard_map/div | solution.py:76
  (6 shorter events, 0.0 us)
Async XLA Ops:
  0.6 5.9 %collective-permute-start = (f32[2048]{0:T(1024)}, f32[2048]{0:T(1024)S(1)}, u32[]{:S(2)}, u32[]{:S(2)}) collective-permute-start(f32[2048]{0:T(1024)} %param.3), channel_id=1, source_target_pairs={{0,1},{1,2},{2,3},{3,0},{4,5},{5,6},{6,7},{7,4},{8,9},{9,10},{10,1... | collective-permute-start | bytes 24584 | tf_op jit(solution)/shard_map/while/body/eval_jaxpr/ppermute | solution.py:46
  1.4 20.2 %collective-permute-start.1 = (bf16[2048,128]{1,0:T(8,128)(2,1)}, bf16[2048,128]{1,0:T(8,128)(2,1)S(1)}, u32[]{:S(2)}, u32[]{:S(2)}) collective-permute-start(bf16[2048,128]{1,0:T(8,128)(2,1)} %param.2), channel_id=1, source_target_pairs={{0,1},{1,2},{2,3},{3,0},{4,5},{5,6},{6,7},{7,4},{8,9},{9,10},{10,1... | collective-permute-start | bytes 1572872 | tf_op jit(solution)/shard_map/while/body/eval_jaxpr/ppermute | solution.py:45
  5.1 26.8 %collective-permute-start.4 = (f32[2048,128]{1,0:T(8,128)}, f32[2048,128]{1,0:T(8,128)S(1)}, u32[]{:S(2)}, u32[]{:S(2)}) collective-permute-start(f32[2048,128]{1,0:T(8,128)} %broadcast_in_dim.13), channel_id=1, source_target_pairs={{0,1},{1,2},{2,3},{3,0},{4,5},{5,6},{6,7},{7,4},{8,9},{9,10},{10,1... | collective-permute-start | bytes 3145736 | tf_op jit(solution)/shard_map/while/body/eval_jaxpr/ppermute | solution.py:47
  6.5 15.1 %copy-start.2 = (f32[2048]{0:T(1024)S(1)}, f32[2048]{0:T(1024)}, u32[]{:S(2)}) copy-start(f32[2048]{0:T(1024)} %param.3) | copy-start | bytes 24580
  6.5 15.5 %copy-start = (bf16[2048,128]{1,0:T(8,128)(2,1)S(1)}, bf16[2048,128]{1,0:T(8,128)(2,1)}, u32[]{:S(2)}) copy-start(bf16[2048,128]{1,0:T(8,128)(2,1)} %param.2) | copy-start | bytes 1572868
  6.5 15.1 %collective-permute-start.2 = (f32[2048]{0:T(1024)S(1)}, f32[2048]{0:T(1024)S(1)}, u32[]{:S(2)}, u32[]{:S(2)}) collective-permute-start(f32[2048]{0:T(1024)S(1)} %collective-permute-done), channel_id=1, source_target_pairs={{0,1},{1,2},{2,3},{3,0},{4,5},{5,6},{6,7},{7,4},{8,9},{9,10},{10,1... | collective-permute-start | bytes 24584 | tf_op jit(solution)/shard_map/ppermute | solution.py:56
  22.0 9.5 %collective-permute-start.3 = (bf16[2048,128]{1,0:T(8,128)(2,1)S(1)}, bf16[2048,128]{1,0:T(8,128)(2,1)S(1)}, u32[]{:S(2)}, u32[]{:S(2)}) collective-permute-start(bf16[2048,128]{1,0:T(8,128)(2,1)S(1)} %collective-permute-done.1), channel_id=1, source_target_pairs={{0,1},{1,2},{2,3},{3,0},{4,5},{5,6},{6,7},{7,4},{8,9},{9,10},{10,1... | collective-permute-start | bytes 1572872 | tf_op jit(solution)/shard_map/ppermute | solution.py:55
  31.5 10.6 %copy-start.1 = (bf16[2048,2048]{0,1:T(8,128)(2,1)}, bf16[2048,2048]{0,1:T(8,128)(2,1)S(1)}, u32[]{:S(2)}) copy-start(bf16[2048,2048]{0,1:T(8,128)(2,1)S(1)} %get-tuple-element.37) | copy-start | bytes 25165828
  34.3 14.3 %collective-permute-start.5 = (f32[2048,128]{1,0:T(8,128)S(1)}, f32[2048,128]{1,0:T(8,128)S(1)}, u32[]{:S(2)}, u32[]{:S(2)}) collective-permute-start(f32[2048,128]{1,0:T(8,128)S(1)} %fusion.15), channel_id=1, source_target_pairs={{0,1},{1,2},{2,3},{3,0},{4,5},{5,6},{6,7},{7,4},{8,9},{9,10},{10,1... | collective-permute-start | bytes 3145736 | tf_op jit(solution)/shard_map/ppermute | solution.py:57
  42.0 10.2 %slice-start = ((s8[8388608]{0:T(1024)(128)(4,1)}), s8[4194304]{0:T(1024)(128)(4,1)S(1)}, s32[]{:S(2)}) async-start(s8[8388608]{0:T(1024)(128)(4,1)} %bitcast.17), calls=%async_computation | async-start | bytes 8388608
  43.4 8.9 %slice-start.1 = ((s8[8388608]{0:T(1024)(128)(4,1)}), s8[4194304]{0:T(1024)(128)(4,1)S(1)}, s32[]{:S(2)}) async-start(s8[8388608]{0:T(1024)(128)(4,1)} %bitcast.17), calls=%async_computation.1 | async-start | bytes 8388608
  49.9 27.0 %collective-permute-start.6 = (f32[2048,128]{1,0:T(8,128)}, f32[2048,128]{1,0:T(8,128)}, u32[]{:S(2)}, u32[]{:S(2)}) collective-permute-start(f32[2048,128]{1,0:T(8,128)} %select_add_fusion), channel_id=1, source_target_pairs={{0,2},{1,3},{2,0},{3,1},{4,6},{5,7},{6,4},{7,5},{8,10},{9,11},{10,... | collective-permute-start | bytes 3145736 | tf_op jit(solution)/shard_map/ppermute | solution.py:74
where the time goes:
time: 80.1 us; the launch traced here: 79.8 us
  matrix products  43.8 us (55%)
  blocking collectives  12.9 us (16%)
  starting transfers between devices  8.28 us (10%)
  other arithmetic  6.52 us (8%)
  waiting for transfers between devices  4.62 us (6%)
  between operations  2.64 us (3%)
  local copies, waits for them, and re-layouts  1.06 us (1%)
    dot_general x3, matrix products, pair_weight(): lax.dot_general(host_x, vis_x, (((1,), (1,)), ((), ())), preferred_elemen...  28.3 us
    psum x1, blocking collectives, device_body(): energy = lax.psum(energy_acc, 'row')  12.9 us
    dot_general x2, matrix products, pair_forces(): jnp.dot(weight_bf, vis_x, preferred_element_type=jnp.float32)  7.99 us
    ppermute x1, waiting for transfers between devices, device_body(): vis_acc = lax.ppermute(vis_acc, 'row', forward)  3.93 us
    dot_general x2, matrix products, pair_forces(): lax.dot_general(weight_bf, host_x, (((0,), (0,)), ((), ())), preferred_el...  3.74 us
    dot_general x1, matrix products, device_body(): jnp.dot(diag_w.astype(jnp.bfloat16), pos_loc, preferred_element_type=jnp....  3.73 us
    div x1, other arithmetic, device_body(): return ((force_acc + home_acc) / ell_sq, energy.reshape(1))  2.98 us
    ppermute x1, starting transfers between devices, full_step(): vis_x = lax.ppermute(vis_x, 'row', forward)  2.6 us
  transfers between devices with their start and end apart: 7, of which 2 were waited for; matrix products, arithmetic and copies ran while one was open for 56% of the time, Pallas kernels for 0%

commit v1 on v0

v1 whole, which is shorter than its diff:
```python
import functools
import math

import jax
import jax.numpy as jnp
from jax import lax
from jax.experimental import pallas as pl
from jax.experimental.pallas import tpu as pltpu
from jax.sharding import PartitionSpec as P

MESH = pl.DeviceIdType.MESH
T = 256
F32 = jnp.float32
BF16 = jnp.bfloat16
PIECE = 64


def split3(v):
    hi = v.astype(BF16).astype(F32)
    rest = v - hi
    mid = rest.astype(BF16).astype(F32)
    return hi, mid, rest - mid


def kernel(rows, feat, chunk, x_ref, q_ref, f_ref, e_ref, xall, qall, aug, xt, qb, rhs, qi, rs, ft, ebuf,
           xsend, xrecv, fsend, frecv, psend, precv, qsend, qrecv, esend, erecv):
    me = lax.axis_index("row")
    partner = me + 1 - 2 * lax.rem(me, 2)
    across = lax.rem(me + 2, 4)
    diagonal = lax.rem(partner + 2, 4)
    peers = (partner, across, diagonal)
    n_chunks = rows // chunk
    tiles = rows // T
    pairs = tiles // 2
    scale = math.log2(math.e) / (2.0 * feat)

    barrier = pltpu.get_barrier_semaphore()
    for peer in peers:
        pl.semaphore_signal(barrier, inc=1, device_id={"row": peer}, device_id_type=MESH)
    pl.semaphore_wait(barrier, 3)

    def remote(src, dst, ssem, rsem, peer):
        return pltpu.make_async_remote_copy(src_ref=src, dst_ref=dst, send_sem=ssem, recv_sem=rsem,
                                            device_id={"row": peer}, device_id_type=MESH)

    q_copies = [remote(q_ref, qall.at[k], qsend.at[k], qrecv.at[k], peer) for k, peer in enumerate(peers)]
    p_copy = remote(x_ref, xall.at[0], psend, precv, partner)
    def x_copy(c):
        part = pl.ds(pl.multiple_of(c * chunk, chunk), chunk)
        return remote(x_ref.at[part], xall.at[1, part], xsend.at[c], xrecv.at[c], across)

    def f_copy(c):
        part = pl.ds(pl.multiple_of(c * chunk, chunk), chunk)
        return remote(xall.at[1, part], xall.at[2, part], fsend.at[c], frecv.at[c], partner)
    for k in (1, 2):
        q_copies[k].start()
    for c in range(n_chunks):
        x_copy(c).start()
    q_copies[0].start()
    p_copy.start()

    row_id = lax.broadcasted_iota(jnp.int32, (8, T), 0)

    def prepare(x_val, q_row, row0, n):
        for k in range(n // T):
            part = x_val[k * T:(k + 1) * T]
            x_t = part.T
            xt[:, pl.ds(row0 + k * T, T)] = x_t
            wide = x_t.astype(F32)
            sq = jnp.sum(wide * wide, axis=0, keepdims=True)
            hi, mid, lo = split3(sq)
            block = jnp.where(row_id == 0, hi, jnp.where(row_id == 1, mid, jnp.where(row_id == 2, lo, jnp.where(row_id < 6, 1.0, 0.0))))
            block = jnp.concatenate([block, jnp.zeros((120, T), F32)], axis=0)
            aug[pl.ds(row0 + k * T, T), :] = block.T.astype(BF16)
            qb[pl.ds(row0 + k * T, T), :] = jnp.broadcast_to(q_row[:, k * T:(k + 1) * T], (128, T)).T
            yield k, x_t, (hi, mid, lo)

    def q_rows(ref):
        return ref[...].reshape(1, rows)

    q_own = q_rows(q_ref)
    qi[...] = jnp.broadcast_to(q_own, (8, rows))
    rs[...] = jnp.zeros_like(rs)
    ft[...] = jnp.zeros_like(ft)
    for k, x_t, (hi, mid, lo) in prepare(x_ref[...], q_own, 0, rows):
        cols = pl.ds(k * T, T)
        rhs[pl.ds(0, feat), cols] = x_t + x_t
        block = jnp.where(row_id < 3, -1.0, jnp.where(row_id == 3, -hi, jnp.where(row_id == 4, -mid, jnp.where(row_id == 5, -lo, 0.0))))
        rhs[pl.ds(feat, 128), cols] = jnp.concatenate([block, jnp.zeros((120, T), F32)], axis=0).astype(BF16)

    def main():
        def first(x_block, row0, t):
            lhs = jnp.concatenate([x_block, aug[pl.ds(row0, T), :]], axis=1)
            return jnp.dot(lhs, rhs[:, 2 * t * T:2 * (t + 1) * T], preferred_element_type=F32)

        def second(s, row0, t, mask_row):
            n = 2 * T
            cols = pl.ds(t * n, n)
            qi_t = qi[:, cols]
            total = rs[:, cols]
            out = []
            for p in range(T // PIECE):
                e = jnp.exp2(jnp.minimum(s[p * PIECE:(p + 1) * PIECE], 0.0) * scale)
                qj = qb[pl.ds(row0 + p * PIECE, PIECE), :]
                qq = (jnp.concatenate([qj] * 4, axis=1).reshape(PIECE // 8, 8, n) * qi_t[None]).reshape(PIECE, n)
                w = qq * e
                if mask_row is not None:
                    r = lax.broadcasted_iota(jnp.int32, (PIECE, n), 0) - lax.broadcasted_iota(jnp.int32, (PIECE, n), 1)
                    w = jnp.where(r == (t * n - p * PIECE) - mask_row, 0.0, w)
                total = total + jnp.sum(w.reshape(PIECE // 8, 8, n), axis=0)
                out.append(w.astype(BF16))
            rs[:, cols] = total
            ft[:, cols] += jnp.dot(xt[:, pl.ds(row0, T)], jnp.concatenate(out, axis=0), preferred_element_type=F32)

        def block_rows(x_of, row0, mask_row=None):
            x_block = x_of()
            ready = first(x_block, row0, 0)
            for t in range(pairs):
                following = first(x_block, row0, t + 1) if t + 1 < pairs else None
                second(ready, row0, t, mask_row)
                ready = following

        def own_step(c, carry):
            off = pl.multiple_of(c * T, T)
            block_rows(lambda: x_ref[pl.ds(off, T), :], off, off)
            return carry
        lax.fori_loop(0, tiles, own_step, 0)

        def other(slot, first_row, n):
            def step(k, carry):
                off = pl.multiple_of(first_row + k * T, T)
                base = pl.multiple_of((slot + 1) * rows + off, T)
                q_row = qall[slot, pl.ds(off // 128, T // 128), :].reshape(1, T)
                for _ in prepare(xall[slot, pl.ds(off, T), :], q_row, base, T):
                    pass
                block_rows(lambda: xall[slot, pl.ds(off, T), :], base)
                return carry
            lax.fori_loop(0, n // T, step, 0)

        q_copies[0].wait_recv()
        p_copy.wait_recv()
        other(0, 0, rows)
        for k in (1, 2):
            q_copies[k].wait_recv()
        def remote_chunk(c, carry):
            x_copy(c).wait_recv()
            f_copy(c).start()
            other(1, c * chunk, chunk)
            return carry
        lax.fori_loop(0, n_chunks, remote_chunk, 0)
        def forwarded_chunk(c, carry):
            f_copy(c).wait_recv()
            other(2, c * chunk, chunk)
            return carry
        lax.fori_loop(0, n_chunks, forwarded_chunk, 0)

        sums = jnp.sum(rs[...], axis=0, keepdims=True)
        energy = 0.5 * jnp.sum(sums, axis=1, keepdims=True)
        ebuf[me] = jnp.broadcast_to(energy, (8, 128))
        inv = 1.0 / feat
        def finish(t, m):
            tile = 2 * t + m
            cols = pl.ds(tile * T, T)
            pulled = ft[:, cols]
            force = (sums[:, tile * T:(tile + 1) * T] * xt[:, cols].astype(F32) - pulled) * inv
            f_ref[pl.ds(tile * T, T), :] = force.T
        finish(0, 0)
        finish(0, 1)
        e_copies = [remote(ebuf.at[me], ebuf.at[me], esend.at[k], erecv.at[k], peer) for k, peer in enumerate(peers)]
        for copy in e_copies:
            copy.start()
        for t in range(1, pairs):
            for m in range(2):
                finish(t, m)
        for copy in e_copies:
            copy.wait_recv()
        everything = (ebuf[0] + ebuf[1]) + (ebuf[2] + ebuf[3])
        e_ref[...] = everything
        for copy in e_copies + q_copies + [p_copy] + [x_copy(c) for c in range(n_chunks)] + [f_copy(c) for c in range(n_chunks)]:
            copy.wait_send()

    main()


def solution(mesh):
    def device_body(pos_loc, chg_loc):
        rows, feat = pos_loc.shape
        chunk = rows // 4
        n = 4
        DMA = pltpu.SemaphoreType.DMA
        call = pl.pallas_call(
            functools.partial(kernel, rows, feat, chunk),
            out_shape=[jax.ShapeDtypeStruct((rows, feat), F32), jax.ShapeDtypeStruct((8, 128), F32)],
            in_specs=[pl.BlockSpec(memory_space=pltpu.VMEM)] * 2,
            out_specs=[pl.BlockSpec(memory_space=pltpu.VMEM)] * 2,
            scratch_shapes=[
                pltpu.VMEM((3, rows, feat), BF16),
                pltpu.VMEM((3, rows // 128, 128), F32),
                pltpu.VMEM((n * rows, 128), BF16),
                pltpu.VMEM((feat, n * rows), BF16),
                pltpu.VMEM((n * rows, 128), F32),
                pltpu.VMEM((2 * 128, rows), BF16),
                pltpu.VMEM((8, rows), F32),
                pltpu.VMEM((8, rows), F32),
                pltpu.VMEM((feat, rows), F32),
                pltpu.VMEM((n, 8, 128), F32),
                DMA((4,)), DMA((4,)), DMA((4,)), DMA((4,)), DMA, DMA, DMA((3,)), DMA((3,)), DMA((3,)), DMA((3,)),
            ],
            compiler_params=pltpu.CompilerParams(collective_id=0, has_side_effects=True, vmem_limit_bytes=48 * 1024 * 1024),
        )
        force, energy = call(pos_loc, chg_loc.reshape(rows // 128, 128))
        return force, energy[0, :1]

    return jax.shard_map(device_body, mesh=mesh, in_specs=(P(("sys", "row"), None), P(("sys", "row"))), out_specs=(P(("sys", "row"), None), P("sys")), check_vma=False)
```

time: 80.1 us -> 45.3 us (0.57)
  matrix products: 43.8 us -> 0 us
  Pallas kernels: 0 us -> 41.2 us
  blocking collectives: 12.9 us -> 0 us
  starting transfers between devices: 8.28 us -> 0 us
  other arithmetic: 6.52 us -> 0 us
  waiting for transfers between devices: 4.62 us -> 0 us
  local copies, waits for them, and re-layouts: 1.06 us -> 3.21 us
  between operations: 2.64 us -> 0.65 us
    dot_general x8 -> x0, matrix products: 43.8 us -> none  [the longest x3 28.3 us: pair_weight(): lax.dot_general(host_x, vis_x, (((1,), (1,)), ((), ())), preferred_elemen...]
    pallas_call x0 -> x1, Pallas kernels: none -> 41.2 us  [device_body(): force, energy = call(pos_loc, chg_loc.reshape(rows // 128, 128))]
    psum x1 -> x0, blocking collectives: 12.9 us -> none  [device_body(): energy = lax.psum(energy_acc, 'row')]
    ppermute x7 -> x0, starting transfers between devices: 8.28 us -> none  [the longest x1 2.6 us: full_step(): vis_x = lax.ppermute(vis_x, 'row', forward)]
    ppermute x7 -> x0, waiting for transfers between devices: 4.62 us -> none  [the longest x1 3.93 us: device_body(): vis_acc = lax.ppermute(vis_acc, 'row', forward)]
    div x1 -> x0, other arithmetic: 2.98 us -> none  [device_body(): return ((force_acc + home_acc) / ell_sq, energy.reshape(1))]
    unnamed x10 -> x5, local copies, waits for them, and re-layouts: 0.02 us -> 2.7 us
    reduce_sum x3 -> x0, other arithmetic: 2.07 us -> none  [row_sq(): return jnp.sum(jnp.square(block_x.astype(jnp.float32)), axis=1)]
  transfers between devices with their start and end apart: 7 -> 0, of which waited for: 2 -> 0; matrix products, arithmetic and copies ran while one was open for 56% -> 0% of each run, Pallas kernels for 0% -> 0%
where the time goes in v1:
time: 45.3 us; the launch traced here: 45.1 us
  Pallas kernels  41.2 us (91%)
  local copies, waits for them, and re-layouts  3.21 us (7%)
  between operations  0.65 us (1%)
    pallas_call x1, Pallas kernels, device_body(): force, energy = call(pos_loc, chg_loc.reshape(rows // 128, 128))  41.2 us
    unnamed x5, local copies, waits for them, and re-layouts  2.7 us

profile of v1, /device:TPU:0, one launch (start us, length us, event | category | flops | bytes accessed | tf_op | source)
XLA Modules:
  0.0 45.1 jit_solution(12980971176330014816)
XLA Ops:
  0.6 0.0 copy-start
  0.6 1.0 %copy-done = bf16[2048,128]{1,0:T(8,128)(2,1)S(1)} copy-done((bf16[2048,128]{1,0:T(8,128)(2,1)S(1)}, bf16[2048,128]{1,0:T(8,128)(2,1)}, u32[]{:S(2)}) %copy-start) | copy-done | bytes 524312
  1.7 0.0 copy-start.1
  1.7 0.7 %copy-done.1 = f32[2048]{0:T(1024)S(1)} copy-done((f32[2048]{0:T(1024)S(1)}, f32[2048]{0:T(1024)}, u32[]{:S(2)}) %copy-start.1) | copy-done | bytes 8216
  2.4 41.2 %shard_map.41 = (f32[2048,128]{1,0:T(8,128)S(1)}, f32[8,128]{1,0:T(8,128)S(1)}) custom-call(bf16[2048,128]{1,0:T(8,128)(2,1)S(1)} %copy-done, f32[16,128]{1,0:T(8,128)S(1)} %bitcast.2), custom_call_target="tpu_custom_call" | custom-call | tf_op jit(solution)/shard_map/pallas_call | solution.py:211
  43.6 0.5 %slice.3 = f32[1,1]{1,0:T(1,128)} slice(f32[8,128]{1,0:T(8,128)S(1)} %get-tuple-element.5), slice={[0:1], [0:1]} | slice | bytes 8 | tf_op jit(solution)/shard_map/slice | solution.py:212
  44.1 1.0 %copy.5 = f32[2048,128]{1,0:T(8,128)} copy(f32[2048,128]{1,0:T(8,128)S(1)} %get-tuple-element.8) | data formatting | bytes 2097152
Async XLA Ops:
  0.6 1.0 %copy-start = (bf16[2048,128]{1,0:T(8,128)(2,1)S(1)}, bf16[2048,128]{1,0:T(8,128)(2,1)}, u32[]{:S(2)}) copy-start(bf16[2048,128]{1,0:T(8,128)(2,1)} %x_ref.1) | copy-start | bytes 1572868
  1.7 0.7 %copy-start.1 = (f32[2048]{0:T(1024)S(1)}, f32[2048]{0:T(1024)}, u32[]{:S(2)}) copy-start(f32[2048]{0:T(1024)} %param.3) | copy-start | bytes 24580

commit v2 on v0

v2 whole, which is shorter than its diff:
```python
import functools
import math

import jax
import jax.numpy as jnp
from jax import lax
from jax.experimental import pallas as pl
from jax.experimental.pallas import tpu as pltpu
from jax.sharding import PartitionSpec as P

MESH = pl.DeviceIdType.MESH
T = 256
F32 = jnp.float32
BF16 = jnp.bfloat16
PIECE = 64


def split3(v):
    hi = v.astype(BF16).astype(F32)
    rest = v - hi
    mid = rest.astype(BF16).astype(F32)
    return hi, mid, rest - mid


def kernel(rows, feat, x_ref, q_ref, f_ref, e_ref, xall, qall, aug, xt, qb, rhs, qi, rs, ft, ebuf,
           xsend, xrecv, fsend, frecv, psend, precv, qsend, qrecv, esend, erecv):
    me = lax.axis_index("row")
    partner = me + 1 - 2 * lax.rem(me, 2)
    across = lax.rem(me + 2, 4)
    diagonal = lax.rem(partner + 2, 4)
    peers = (partner, across, diagonal)
    chunk = 2 * T
    n_chunks = rows // chunk
    lanes = chunk // 128
    scale = math.log2(math.e) / (2.0 * feat)

    barrier = pltpu.get_barrier_semaphore()
    for peer in peers:
        pl.semaphore_signal(barrier, inc=1, device_id={"row": peer}, device_id_type=MESH)
    pl.semaphore_wait(barrier, 3)

    def remote(src, dst, ssem, rsem, peer):
        return pltpu.make_async_remote_copy(src_ref=src, dst_ref=dst, send_sem=ssem, recv_sem=rsem,
                                            device_id={"row": peer}, device_id_type=MESH)

    def part(c):
        return pl.ds(pl.multiple_of(c * chunk, chunk), chunk)

    q_copies = [remote(q_ref, qall.at[k], qsend.at[k], qrecv.at[k], peer) for k, peer in enumerate(peers)]

    def p_copy(c):
        return remote(x_ref.at[part(c)], xall.at[0, part(c)], psend.at[c], precv.at[c], partner)

    def x_copy(c):
        return remote(x_ref.at[part(c)], xall.at[1, part(c)], xsend.at[c], xrecv.at[c], across)

    def f_copy(c):
        return remote(xall.at[1, part(c)], xall.at[2, part(c)], fsend.at[c], frecv.at[c], partner)

    for k in (1, 2, 0):
        q_copies[k].start()
    for c in range(n_chunks):
        x_copy(c).start()
        p_copy(c).start()

    row_id = lax.broadcasted_iota(jnp.int32, (8, chunk), 0)
    filler = jnp.zeros((120, chunk), BF16)

    def prepare(x_val, q_row, g):
        x_t = x_val.T
        for k in range(lanes):
            xt[g * lanes + k] = x_t[:, k * 128:(k + 1) * 128]
        wide = x_t.astype(F32)
        hi, mid, lo = split3(jnp.sum(wide * wide, axis=0, keepdims=True))
        block = jnp.where(row_id == 0, hi, jnp.where(row_id == 1, mid, jnp.where(row_id == 2, lo, jnp.where(row_id < 6, 1.0, 0.0))))
        aug[g] = jnp.concatenate([block, jnp.zeros((120, chunk), F32)], axis=0).astype(BF16).T
        qb[g] = jnp.broadcast_to(q_row, (128, chunk)).T
        return x_t, hi, mid, lo

    def q_rows(ref, c):
        return ref[pl.ds(c * lanes, lanes), :].reshape(1, chunk)

    rs[...] = jnp.zeros_like(rs)
    ft[...] = jnp.zeros_like(ft)
    for c in range(n_chunks):
        q_row = q_rows(q_ref, c)
        qi[c] = jnp.broadcast_to(q_row, (8, chunk))
        x_t, hi, mid, lo = prepare(x_ref[pl.ds(c * chunk, chunk), :], q_row, c)
        block = jnp.where(row_id < 3, -1.0, jnp.where(row_id == 3, -hi, jnp.where(row_id == 4, -mid, jnp.where(row_id == 5, -lo, 0.0))))
        block = jnp.concatenate([block, jnp.zeros((120, chunk), F32)], axis=0).astype(BF16)
        double = x_t + x_t
        for k in range(lanes):
            rhs[c, k, pl.ds(0, feat), :] = double[:, k * 128:(k + 1) * 128]
            rhs[c, k, pl.ds(feat, 128), :] = block[:, k * 128:(k + 1) * 128]

    def wide_load(ref, i):
        return jnp.concatenate([ref[i, k] for k in range(lanes)], axis=1)

    def first(x_of, g, h, t):
        lhs = jnp.concatenate([x_of(h), aug[g, pl.ds(h * T, T), :]], axis=1)
        return jnp.dot(lhs, wide_load(rhs, t), preferred_element_type=F32)

    def weights(s, g, h, t, masked):
        qi_t = qi[t]
        total = rs[t]
        out = []
        for p in range(T // PIECE):
            e = jnp.exp2(jnp.minimum(s[p * PIECE:(p + 1) * PIECE], 0.0) * scale)
            qj = qb[g, pl.ds(h * T + p * PIECE, PIECE), :]
            qq = (jnp.concatenate([qj] * lanes, axis=1).reshape(PIECE // 8, 8, chunk) * qi_t[None]).reshape(PIECE, chunk)
            w = qq * e
            if masked:
                r = lax.broadcasted_iota(jnp.int32, (PIECE, chunk), 0) + (h * T + p * PIECE)
                w = jnp.where(r == lax.broadcasted_iota(jnp.int32, (PIECE, chunk), 1), 0.0, w)
            total = total + jnp.sum(w.reshape(PIECE // 8, 8, chunk), axis=0)
            out.append(w.astype(BF16))
        rs[t] = total
        return jnp.concatenate(out, axis=0)

    def chunk_rows(x_of, g, groups):
        steps = [(t, h, m) for t, m in groups for h in range(2)]
        ready = first(x_of, g, steps[0][1], steps[0][0])
        got = []
        for n, (t, h, m) in enumerate(steps):
            following = first(x_of, g, steps[n + 1][1], steps[n + 1][0]) if n + 1 < len(steps) else None
            got.append(weights(ready, g, h, t, m))
            if h == 1:
                lhs = jnp.concatenate([xt[g * lanes + k] for k in range(lanes)], axis=1)
                ft[t] += jnp.dot(lhs, jnp.concatenate(got, axis=0), preferred_element_type=F32)
                got = []
            ready = following

    def arrive(slot, c):
        if slot == 0:
            p_copy(c).wait_recv()
        elif slot == 1:
            x_copy(c).wait_recv()
            f_copy(c).start()
        else:
            f_copy(c).wait_recv()

    for slot in range(n_chunks):
        for k in ((0,), (1, 2), (), ())[slot]:
            q_copies[k].wait_recv()

        def body(c, carry, slot=slot):
            if slot < 3:
                arrive(slot, c)
                prepare(xall[slot, part(c), :], q_rows(qall.at[slot], c), (slot + 1) * n_chunks + c)
            if slot == 0:
                x_of = lambda h: x_ref[pl.ds(pl.multiple_of(c * chunk + h * T, T), T), :]
                groups = [(lax.rem(c + k, n_chunks), k == 0) for k in range(n_chunks)]
            else:
                x_of = lambda h: xall[slot - 1, pl.ds(pl.multiple_of(c * chunk + h * T, T), T), :]
                groups = [(k, False) for k in range(n_chunks)]
            chunk_rows(x_of, slot * n_chunks + c, groups)
            return carry
        lax.fori_loop(0, n_chunks, body, 0)

    sums = [jnp.sum(rs[t], axis=0, keepdims=True) for t in range(n_chunks)]
    energy = 0.5 * jnp.sum((sums[0] + sums[1]) + (sums[2] + sums[3]), axis=1, keepdims=True)
    ebuf[me] = jnp.broadcast_to(energy, (8, 128))
    inv = 1.0 / feat

    def finish(t):
        own = jnp.concatenate([xt[t * lanes + k] for k in range(lanes)], axis=1).astype(F32)
        f_ref[pl.ds(t * chunk, chunk), :] = ((sums[t] * own - ft[t]) * inv).T

    finish(0)
    e_copies = [remote(ebuf.at[me], ebuf.at[me], esend.at[k], erecv.at[k], peer) for k, peer in enumerate(peers)]
    for copy in e_copies:
        copy.start()
    for t in range(1, n_chunks):
        finish(t)
    for copy in e_copies:
        copy.wait_recv()
    e_ref[...] = (ebuf[0] + ebuf[1]) + (ebuf[2] + ebuf[3])
    for copy in e_copies + q_copies + [f(c) for f in (p_copy, x_copy, f_copy) for c in range(n_chunks)]:
        copy.wait_send()


def solution(mesh):
    def device_body(pos_loc, chg_loc):
        rows, feat = pos_loc.shape
        chunk, n = 2 * T, 4
        own = rows // chunk
        DMA = pltpu.SemaphoreType.DMA
        call = pl.pallas_call(
            functools.partial(kernel, rows, feat),
            out_shape=[jax.ShapeDtypeStruct((rows, feat), F32), jax.ShapeDtypeStruct((8, 128), F32)],
            in_specs=[pl.BlockSpec(memory_space=pltpu.VMEM)] * 2,
            out_specs=[pl.BlockSpec(memory_space=pltpu.VMEM)] * 2,
            scratch_shapes=[
                pltpu.VMEM((3, rows, feat), BF16),
                pltpu.VMEM((3, rows // 128, 128), F32),
                pltpu.VMEM((n * own, chunk, 128), BF16),
                pltpu.VMEM((n * rows // 128, feat, 128), BF16),
                pltpu.VMEM((n * own, chunk, 128), F32),
                pltpu.VMEM((own, chunk // 128, 2 * 128, 128), BF16),
                pltpu.VMEM((own, 8, chunk), F32),
                pltpu.VMEM((own, 8, chunk), F32),
                pltpu.VMEM((own, feat, chunk), F32),
                pltpu.VMEM((n, 8, 128), F32),
                DMA((own,)), DMA((own,)), DMA((own,)), DMA((own,)), DMA((own,)), DMA((own,)), DMA((3,)), DMA((3,)), DMA((3,)), DMA((3,)),
            ],
            compiler_params=pltpu.CompilerParams(collective_id=0, has_side_effects=True, vmem_limit_bytes=48 * 1024 * 1024),
        )
        force, energy = call(pos_loc, chg_loc.reshape(rows // 128, 128))
        return force, energy[0, :1]

    return jax.shard_map(device_body, mesh=mesh, in_specs=(P(("sys", "row"), None), P(("sys", "row"))), out_specs=(P(("sys", "row"), None), P("sys")), check_vma=False)
```

time: 80.1 us -> 38.1 us (0.48)
  matrix products: 43.8 us -> 0 us
  Pallas kernels: 0 us -> 34 us
  blocking collectives: 12.9 us -> 0 us
  starting transfers between devices: 8.28 us -> 0 us
  other arithmetic: 6.52 us -> 0 us
  waiting for transfers between devices: 4.62 us -> 0 us
  local copies, waits for them, and re-layouts: 1.06 us -> 3.21 us
  between operations: 2.64 us -> 0.65 us
    dot_general x8 -> x0, matrix products: 43.8 us -> none  [the longest x3 28.3 us: pair_weight(): lax.dot_general(host_x, vis_x, (((1,), (1,)), ((), ())), preferred_elemen...]
    pallas_call x0 -> x1, Pallas kernels: none -> 34 us  [device_body(): force, energy = call(pos_loc, chg_loc.reshape(rows // 128, 128))]
    psum x1 -> x0, blocking collectives: 12.9 us -> none  [device_body(): energy = lax.psum(energy_acc, 'row')]
    ppermute x7 -> x0, starting transfers between devices: 8.28 us -> none  [the longest x1 2.6 us: full_step(): vis_x = lax.ppermute(vis_x, 'row', forward)]
    ppermute x7 -> x0, waiting for transfers between devices: 4.62 us -> none  [the longest x1 3.93 us: device_body(): vis_acc = lax.ppermute(vis_acc, 'row', forward)]
    div x1 -> x0, other arithmetic: 2.98 us -> none  [device_body(): return ((force_acc + home_acc) / ell_sq, energy.reshape(1))]
    unnamed x10 -> x5, local copies, waits for them, and re-layouts: 0.02 us -> 2.7 us
    reduce_sum x3 -> x0, other arithmetic: 2.07 us -> none  [row_sq(): return jnp.sum(jnp.square(block_x.astype(jnp.float32)), axis=1)]
  transfers between devices with their start and end apart: 7 -> 0, of which waited for: 2 -> 0; matrix products, arithmetic and copies ran while one was open for 56% -> 0% of each run, Pallas kernels for 0% -> 0%
where the time goes in v2:
time: 38.1 us; the launch traced here: 37.9 us
  Pallas kernels  34 us (89%)
  local copies, waits for them, and re-layouts  3.21 us (8%)
  between operations  0.65 us (2%)
    pallas_call x1, Pallas kernels, device_body(): force, energy = call(pos_loc, chg_loc.reshape(rows // 128, 128))  34 us
    unnamed x5, local copies, waits for them, and re-layouts  2.7 us

profile of v2, /device:TPU:0, one launch (start us, length us, event | category | flops | bytes accessed | tf_op | source)
XLA Modules:
  0.0 37.9 jit_solution(13869070893663377992)
XLA Ops:
  0.6 0.0 copy-start
  0.6 1.0 %copy-done = bf16[2048,128]{1,0:T(8,128)(2,1)S(1)} copy-done((bf16[2048,128]{1,0:T(8,128)(2,1)S(1)}, bf16[2048,128]{1,0:T(8,128)(2,1)}, u32[]{:S(2)}) %copy-start) | copy-done | bytes 524312
  1.7 0.0 copy-start.1
  1.7 0.7 %copy-done.1 = f32[2048]{0:T(1024)S(1)} copy-done((f32[2048]{0:T(1024)S(1)}, f32[2048]{0:T(1024)}, u32[]{:S(2)}) %copy-start.1) | copy-done | bytes 8216
  2.4 34.0 %shard_map.41 = (f32[2048,128]{1,0:T(8,128)S(1)}, f32[8,128]{1,0:T(8,128)S(1)}) custom-call(bf16[2048,128]{1,0:T(8,128)(2,1)S(1)} %copy-done, f32[16,128]{1,0:T(8,128)S(1)} %bitcast.2), custom_call_target="tpu_custom_call" | custom-call | tf_op jit(solution)/shard_map/pallas_call | solution.py:208
  36.4 0.5 %slice.3 = f32[1,1]{1,0:T(1,128)} slice(f32[8,128]{1,0:T(8,128)S(1)} %get-tuple-element.5), slice={[0:1], [0:1]} | slice | bytes 8 | tf_op jit(solution)/shard_map/slice | solution.py:209
  36.9 1.0 %copy.5 = f32[2048,128]{1,0:T(8,128)} copy(f32[2048,128]{1,0:T(8,128)S(1)} %get-tuple-element.8) | data formatting | bytes 2097152
Async XLA Ops:
  0.6 1.0 %copy-start = (bf16[2048,128]{1,0:T(8,128)(2,1)S(1)}, bf16[2048,128]{1,0:T(8,128)(2,1)}, u32[]{:S(2)}) copy-start(bf16[2048,128]{1,0:T(8,128)(2,1)} %x_ref.1) | copy-start | bytes 1572868
  1.7 0.7 %copy-start.1 = (f32[2048]{0:T(1024)S(1)}, f32[2048]{0:T(1024)}, u32[]{:S(2)}) copy-start(f32[2048]{0:T(1024)} %param.3) | copy-start | bytes 24580

commit v3 on v2

v3 whole, which is shorter than its diff:
```python
import functools
import math

import jax
import jax.numpy as jnp
from jax import lax
from jax.experimental import pallas as pl
from jax.experimental.pallas import tpu as pltpu
from jax.sharding import PartitionSpec as P

MESH = pl.DeviceIdType.MESH
T = 256
F32 = jnp.float32
BF16 = jnp.bfloat16
PIECE = 64


def split3(v):
    hi = v.astype(BF16).astype(F32)
    rest = v - hi
    mid = rest.astype(BF16).astype(F32)
    return hi, mid, rest - mid


def kernel(rows, feat, x_ref, q_ref, f_ref, e_ref, xall, qall, aug, xt, qb, rhs, qi, rs, ft, sbuf, wbuf, ebuf,
           lsem, xsend, xrecv, fsend, frecv, psend, precv, qsend, qrecv, esend, erecv):
    me = lax.axis_index("row")
    upper = me // 2
    partner = me + 1 - 2 * lax.rem(me, 2)
    third = (1 - upper) * (3 - me) + upper * (me - 2)
    last = third + 1 - 2 * lax.rem(third, 2)
    peers = (partner, third, last)
    chunk = 2 * T
    own = rows // chunk
    total = 4 * own
    half = own // 2
    lanes = chunk // 128
    scale = math.log2(math.e) / (2.0 * feat)

    local = [pltpu.make_async_copy(q_ref, qall.at[pl.ds(0, own * lanes)], lsem.at[own])]
    local += [pltpu.make_async_copy(x_ref.at[c], xall.at[c], lsem.at[c]) for c in range(own)]
    for copy in local:
        copy.start()
    barrier = pltpu.get_barrier_semaphore()
    for peer in peers:
        pl.semaphore_signal(barrier, inc=1, device_id={"row": peer}, device_id_type=MESH)

    def remote(src, dst, ssem, rsem, peer):
        return pltpu.make_async_remote_copy(src_ref=src, dst_ref=dst, send_sem=ssem, recv_sem=rsem,
                                            device_id={"row": peer}, device_id_type=MESH)

    q_copies = [remote(q_ref, qall.at[pl.ds((k + 1) * own * lanes, own * lanes)], qsend.at[k], qrecv.at[k], peer)
                for k, peer in enumerate(peers)]
    p_copy = remote(xall.at[pl.ds(0, own)], xall.at[pl.ds(own, own)], psend, precv, partner)
    x_copies = [remote(xall.at[pl.ds(k * half, half)], xall.at[pl.ds(2 * own + k * half, half)], xsend.at[k], xrecv.at[k], third)
                for k in range(2)]
    f_copies = [remote(xall.at[pl.ds(2 * own + k * half, half)], xall.at[pl.ds(3 * own + k * half, half)], fsend.at[k], frecv.at[k], partner)
                for k in range(2)]

    row_id = lax.broadcasted_iota(jnp.int32, (8, chunk), 0)
    filler = jnp.zeros((120, chunk), F32)

    def norms(x_t):
        wide = x_t.astype(F32)
        return split3(jnp.sum(wide * wide, axis=0, keepdims=True))

    def q_row(g):
        return qall[pl.ds(g * lanes, lanes), :].reshape(1, chunk)

    def prepare(g, side):
        x_t = xall[g].T
        hi, mid, lo = norms(x_t)
        block = jnp.where(row_id == 0, hi, jnp.where(row_id == 1, mid, jnp.where(row_id == 2, lo, jnp.where(row_id < 6, 1.0, 0.0))))
        aug[side] = jnp.concatenate([block, filler], axis=0).astype(BF16).T
        qb[side] = jnp.broadcast_to(q_row(g), (128, chunk)).T
        for k in range(lanes):
            xt[side, k] = x_t[:, k * 128:(k + 1) * 128]

    def wide_load(ref, i):
        return jnp.concatenate([ref[i, k] for k in range(lanes)], axis=1)

    def first(g, side, h, t):
        lhs = jnp.concatenate([xall[g, pl.ds(h * T, T), :], aug[side, pl.ds(h * T, T), :]], axis=1)
        return jnp.dot(lhs, wide_load(rhs, t), preferred_element_type=F32)

    def weights(s, side, h, t, phase, masked, keep):
        qi_t = qi[t]
        acc = rs[phase, t]
        for p in range(T // PIECE):
            e = jnp.exp2(jnp.minimum(s(p), 0.0) * scale)
            rows_p = pl.ds(h * T + p * PIECE, PIECE)
            qj = qb[side, rows_p, :]
            qq = (jnp.concatenate([qj] * lanes, axis=1).reshape(PIECE // 8, 8, chunk) * qi_t[None]).reshape(PIECE, chunk)
            w = qq * e
            if masked:
                r = lax.broadcasted_iota(jnp.int32, (PIECE, chunk), 0) + (h * T + p * PIECE)
                w = jnp.where(r == lax.broadcasted_iota(jnp.int32, (PIECE, chunk), 1), 0.0, w)
            acc = acc + jnp.sum(w.reshape(PIECE // 8, 8, chunk), axis=0)
            w = w.astype(BF16)
            for j in range(lanes):
                wbuf[keep, j, rows_p, :] = w[:, j * 128:(j + 1) * 128]
        rs[phase, t] = acc

    def pull(side, t, keep):
        ft[t] += jnp.dot(wide_load(xt, side), wide_load(wbuf, keep), preferred_element_type=F32)

    def body(g, side, order, before, phase, masked=False, prep=True):
        steps = [(k, h) for k in range(own) for h in range(2)]
        ready = lambda p: sbuf[pl.ds(p * PIECE, PIECE), :]
        for n, (k, h) in enumerate(steps):
            if n + 1 < len(steps):
                following = first(g, side, steps[n + 1][1], order[steps[n + 1][0]])
            if h == 0:
                if k == 0:
                    pull(1 - side, before, 1)
                else:
                    pull(side, order[k - 1], (k - 1) % 2)
            if n == 0 and prep:
                prepare(g + 1, 1 - side)
            weights(ready, side, h, order[k], phase, masked and k == 0, k % 2)
            ready = lambda p, v=following: v[p * PIECE:(p + 1) * PIECE]
        if prep:
            sbuf[...] = first(g + 1, 1 - side, 0, prep[0] if isinstance(prep, list) else 0)

    rs[...] = jnp.zeros_like(rs)
    ft[...] = jnp.zeros_like(ft)
    wbuf[1] = jnp.zeros_like(wbuf[1])
    xt[1] = jnp.zeros_like(xt[1])
    local[0].wait()
    for c in range(own):
        local[1 + c].wait()
        qi[c] = jnp.broadcast_to(q_row(c), (8, chunk))
        x_t = xall[c].T
        hi, mid, lo = norms(x_t)
        block = jnp.where(row_id < 3, -1.0, jnp.where(row_id == 3, -hi, jnp.where(row_id == 4, -mid, jnp.where(row_id == 5, -lo, 0.0))))
        block = jnp.concatenate([block, filler], axis=0).astype(BF16)
        double = x_t + x_t
        for k in range(lanes):
            rhs[c, k, pl.ds(0, feat), :] = double[:, k * 128:(k + 1) * 128]
            rhs[c, k, pl.ds(feat, 128), :] = block[:, k * 128:(k + 1) * 128]
    prepare(0, 0)
    sbuf[...] = first(0, 0, 0, 0)

    pl.semaphore_wait(barrier, 3)
    for k in (1, 2, 0):
        q_copies[k].start()
    for copy in x_copies + [p_copy]:
        copy.start()

    fixed = list(range(own))
    for g in range(own):
        if g == own - 1:
            q_copies[0].wait_recv()
            p_copy.wait_recv()
        body(g, g % 2, fixed[g:] + fixed[:g], (g + own - 2) % own, 0, masked=True, prep=[(g + 1) % own])

    def two(i, carry, phase, before):
        g = own + 2 * i
        body(g, 0, fixed, own - 1, phase)
        @pl.when(g + 1 == 2 * own - 1)
        def _():
            q_copies[1].wait_recv()
            q_copies[2].wait_recv()
            x_copies[0].wait_recv()
            f_copies[0].start()

        @pl.when(g + 1 == 2 * own + half - 1)
        def _():
            x_copies[1].wait_recv()
            f_copies[1].start()
        @pl.when(g + 1 == 3 * own - 1)
        def _():
            f_copies[0].wait_recv()
        body(g + 1, 1, fixed, own - 1, phase)
        return carry
    body(own, 0, fixed, own - 2, 0)
    body(own + 1, 1, fixed, own - 1, 0)
    lax.fori_loop(1, own, lambda i, c: two(i, c, i // half, None), 0)

    def total_of(phase):
        sums = (rs[phase, 0] + rs[phase, 1]) + (rs[phase, 2] + rs[phase, 3])
        return jnp.sum(jnp.sum(sums, axis=0, keepdims=True), axis=1, keepdims=True)
    ebuf[me] = jnp.broadcast_to(0.5 * total_of(0) + total_of(1), (8, 128))
    e_copies = [remote(ebuf.at[me], ebuf.at[me], esend.at[k], erecv.at[k], peer) for k, peer in enumerate(peers)]

    for g in range(3 * own, total):
        if g == 3 * own + half - 1:
            f_copies[1].wait_recv()
        if g == 3 * own + half:
            for copy in e_copies:
                copy.start()
        body(g, g % 2, fixed, own - 1, 2, prep=g + 1 < total)
    pull(1, own - 1, 1)

    inv = 1.0 / feat
    for t in range(own):
        sums = jnp.sum(rs[0, t] + rs[1, t] + rs[2, t], axis=0, keepdims=True)
        mine = xall[t].T.astype(F32)
        f_ref[pl.ds(t * chunk, chunk), :] = ((sums * mine - ft[t]) * inv).T
    for copy in e_copies:
        copy.wait_recv()
    e_ref[...] = (ebuf[0] + ebuf[1]) + (ebuf[2] + ebuf[3])
    for copy in e_copies + q_copies + [p_copy] + x_copies + f_copies:
        copy.wait_send()


def solution(mesh):
    def device_body(pos_loc, chg_loc):
        rows, feat = pos_loc.shape
        chunk = 2 * T
        own = rows // chunk
        total = 4 * own
        DMA = pltpu.SemaphoreType.DMA
        call = pl.pallas_call(
            functools.partial(kernel, rows, feat),
            out_shape=[jax.ShapeDtypeStruct((rows, feat), F32), jax.ShapeDtypeStruct((8, 128), F32)],
            in_specs=[pl.BlockSpec(memory_space=pl.ANY)] * 2,
            out_specs=[pl.BlockSpec(memory_space=pltpu.VMEM)] * 2,
            scratch_shapes=[
                pltpu.VMEM((total, chunk, feat), BF16),
                pltpu.VMEM((4 * rows // 128, 128), F32),
                pltpu.VMEM((2, chunk, 128), BF16),
                pltpu.VMEM((2, chunk // 128, feat, 128), BF16),
                pltpu.VMEM((2, chunk, 128), F32),
                pltpu.VMEM((own, chunk // 128, 2 * 128, 128), BF16),
                pltpu.VMEM((own, 8, chunk), F32),
                pltpu.VMEM((3, own, 8, chunk), F32),
                pltpu.VMEM((own, feat, chunk), F32),
                pltpu.VMEM((T, chunk), F32),
                pltpu.VMEM((2, chunk // 128, chunk, 128), BF16),
                pltpu.VMEM((4, 8, 128), F32),
                DMA((own + 1,)), DMA((2,)), DMA((2,)), DMA((2,)), DMA((2,)), DMA, DMA, DMA((3,)), DMA((3,)), DMA((3,)), DMA((3,)),
            ],
            compiler_params=pltpu.CompilerParams(collective_id=0, has_side_effects=True, vmem_limit_bytes=48 * 1024 * 1024),
        )
        force, energy = call(pltpu.with_memory_space_constraint(pos_loc.reshape(own, chunk, feat), pltpu.HBM),
                             pltpu.with_memory_space_constraint(chg_loc.reshape(rows // 128, 128), pltpu.HBM))
        return force, energy[0, :1]

    return jax.shard_map(device_body, mesh=mesh, in_specs=(P(("sys", "row"), None), P(("sys", "row"))), out_specs=(P(("sys", "row"), None), P("sys")), check_vma=False)
```

time: 38.1 us -> 29.7 us (0.78)
  Pallas kernels: 34 us -> 27.4 us
  local copies, waits for them, and re-layouts: 3.21 us -> 1.48 us
    pallas_call x1, Pallas kernels: 34 us -> 27.4 us  [device_body(): call(pltpu.with_memory_space_constraint(pos_loc.reshape(own, chunk, feat)...]
    unnamed x5 -> x1, local copies, waits for them, and re-layouts: 2.7 us -> 0.97 us
where the time goes in v3:
time: 29.7 us; the launch traced here: 29.5 us
  Pallas kernels  27.4 us (92%)
  local copies, waits for them, and re-layouts  1.48 us (5%)
  between operations  0.64 us (2%)
    pallas_call x1, Pallas kernels, device_body(): call(pltpu.with_memory_space_constraint(pos_loc.reshape(own, chunk, feat)...  27.4 us
    unnamed x1, local copies, waits for them, and re-layouts  0.97 us

profile of v3, /device:TPU:0, one launch (start us, length us, event | category | flops | bytes accessed | tf_op | source)
XLA Modules:
  0.0 29.5 jit_solution(11525050508431392817)
XLA Ops:
  0.6 27.4 %shard_map.41 = (f32[2048,128]{1,0:T(8,128)S(1)}, f32[8,128]{1,0:T(8,128)S(1)}) custom-call(bf16[4,512,128]{2,1,0:T(8,128)(2,1)} %bitcast.3, f32[16,128]{1,0:T(8,128)} %bitcast.4), custom_call_target="tpu_custom_call" | custom-call | tf_op jit(solution)/shard_map/pallas_call | solution.py:236
  28.0 0.5 %slice.3 = f32[1,1]{1,0:T(1,128)} slice(f32[8,128]{1,0:T(8,128)S(1)} %get-tuple-element.5), slice={[0:1], [0:1]} | slice | bytes 8 | tf_op jit(solution)/shard_map/slice | solution.py:238
  28.5 1.0 %copy.5 = f32[2048,128]{1,0:T(8,128)} copy(f32[2048,128]{1,0:T(8,128)S(1)} %get-tuple-element.8) | data formatting | bytes 2097152

commit v4 on v3

--- a/solution.py
+++ b/solution.py
@@ -22,7 +22,7 @@
     return hi, mid, rest - mid
 
 
-def kernel(rows, feat, x_ref, q_ref, f_ref, e_ref, xall, qall, aug, xt, qb, rhs, qi, rs, ft, sbuf, wbuf, ebuf,
+def kernel(rows, feat, x_ref, q_ref, ft, rs, ebuf, xall, qall, aug, xt, qb, rhs, top, sign, sbuf, wbuf,
            lsem, xsend, xrecv, fsend, frecv, psend, precv, qsend, qrecv, esend, erecv):
     me = lax.axis_index("row")
     upper = me // 2
@@ -84,14 +84,12 @@
         return jnp.dot(lhs, wide_load(rhs, t), preferred_element_type=F32)
 
     def weights(s, side, h, t, phase, masked, keep):
-        qi_t = qi[t]
+        top_t = top[t]
         acc = rs[phase, t]
         for p in range(T // PIECE):
-            e = jnp.exp2(jnp.minimum(s(p), 0.0) * scale)
+            e = jnp.exp2(jnp.minimum(s(p).reshape(PIECE // 8, 8, chunk), top_t[None]) * scale).reshape(PIECE, chunk)
             rows_p = pl.ds(h * T + p * PIECE, PIECE)
-            qj = qb[side, rows_p, :]
-            qq = (jnp.concatenate([qj] * lanes, axis=1).reshape(PIECE // 8, 8, chunk) * qi_t[None]).reshape(PIECE, chunk)
-            w = qq * e
+            w = jnp.concatenate([qb[side, rows_p, :]] * lanes, axis=1) * e
             if masked:
                 r = lax.broadcasted_iota(jnp.int32, (PIECE, chunk), 0) + (h * T + p * PIECE)
                 w = jnp.where(r == lax.broadcasted_iota(jnp.int32, (PIECE, chunk), 1), 0.0, w)
@@ -129,10 +127,15 @@
     local[0].wait()
     for c in range(own):
         local[1 + c].wait()
-        qi[c] = jnp.broadcast_to(q_row(c), (8, chunk))
+        q_c = q_row(c)
+        sign[c] = jnp.broadcast_to(jnp.where(q_c < 0.0, -1.0, 1.0), (8, chunk))
+        level = jnp.maximum(jnp.log2(jnp.abs(q_c)), -1000.0) * (1.0 / scale)
+        top[c] = jnp.broadcast_to(level, (8, chunk))
         x_t = xall[c].T
-        hi, mid, lo = norms(x_t)
-        block = jnp.where(row_id < 3, -1.0, jnp.where(row_id == 3, -hi, jnp.where(row_id == 4, -mid, jnp.where(row_id == 5, -lo, 0.0))))
+        terms = [-1.0, -1.0, -1.0] + [v for v in split3(level - jnp.sum(jnp.square(x_t.astype(F32)), axis=0, keepdims=True))]
+        block = jnp.zeros((8, chunk), F32)
+        for k, v in enumerate(terms):
+            block = jnp.where(row_id == k, v, block)
         block = jnp.concatenate([block, filler], axis=0).astype(BF16)
         double = x_t + x_t
         for k in range(lanes):
@@ -178,7 +181,7 @@
     lax.fori_loop(1, own, lambda i, c: two(i, c, i // half, None), 0)
 
     def total_of(phase):
-        sums = (rs[phase, 0] + rs[phase, 1]) + (rs[phase, 2] + rs[phase, 3])
+        sums = (rs[phase, 0] * sign[0] + rs[phase, 1] * sign[1]) + (rs[phase, 2] * sign[2] + rs[phase, 3] * sign[3])
         return jnp.sum(jnp.sum(sums, axis=0, keepdims=True), axis=1, keepdims=True)
     ebuf[me] = jnp.broadcast_to(0.5 * total_of(0) + total_of(1), (8, 128))
     e_copies = [remote(ebuf.at[me], ebuf.at[me], esend.at[k], erecv.at[k], peer) for k, peer in enumerate(peers)]
@@ -192,16 +195,29 @@
         body(g, g % 2, fixed, own - 1, 2, prep=g + 1 < total)
     pull(1, own - 1, 1)
 
-    inv = 1.0 / feat
     for t in range(own):
-        sums = jnp.sum(rs[0, t] + rs[1, t] + rs[2, t], axis=0, keepdims=True)
-        mine = xall[t].T.astype(F32)
-        f_ref[pl.ds(t * chunk, chunk), :] = ((sums * mine - ft[t]) * inv).T
+        rs[0, t] = (rs[0, t] + rs[1, t]) + rs[2, t]
+        rs[1, t] = sign[t]
     for copy in e_copies:
         copy.wait_recv()
-    e_ref[...] = (ebuf[0] + ebuf[1]) + (ebuf[2] + ebuf[3])
     for copy in e_copies + q_copies + [p_copy] + x_copies + f_copies:
         copy.wait_send()
+
+
+def finish(x_ref, ft, rs, ebuf, f_ref, e_ref, stage, sems):
+    own, feat, chunk = ft.shape
+    inv = 1.0 / feat
+    copies = []
+    for t in range(own):
+        factor = rs[1, t, pl.ds(0, 1), :] * inv
+        sums = jnp.sum(rs[0, t], axis=0, keepdims=True)
+        stage[t] = ((sums * x_ref[t].T.astype(F32) - ft[t]) * factor).T
+        copies.append(pltpu.make_async_copy(stage.at[t], f_ref.at[t], sems.at[t]))
+        copies[-1].start()
+    energy = (ebuf[0] + ebuf[1]) + (ebuf[2] + ebuf[3])
+    e_ref[0] = jnp.max(energy[0:1, 0:1])
+    for copy in copies:
+        copy.wait()
 
 
 def solution(mesh):
@@ -213,9 +229,10 @@
         DMA = pltpu.SemaphoreType.DMA
         call = pl.pallas_call(
             functools.partial(kernel, rows, feat),
-            out_shape=[jax.ShapeDtypeStruct((rows, feat), F32), jax.ShapeDtypeStruct((8, 128), F32)],
+            out_shape=[jax.ShapeDtypeStruct((own, feat, chunk), F32), jax.ShapeDtypeStruct((3, own, 8, chunk), F32),
+                       jax.ShapeDtypeStruct((4, 8, 128), F32)],
             in_specs=[pl.BlockSpec(memory_space=pl.ANY)] * 2,
-            out_specs=[pl.BlockSpec(memory_space=pltpu.VMEM)] * 2,
+            out_specs=[pl.BlockSpec(memory_space=pltpu.VMEM)] * 3,
             scratch_shapes=[
                 pltpu.VMEM((total, chunk, feat), BF16),
                 pltpu.VMEM((4 * rows // 128, 128), F32),
@@ -224,17 +241,24 @@
                 pltpu.VMEM((2, chunk, 128), F32),
                 pltpu.VMEM((own, chunk // 128, 2 * 128, 128), BF16),
                 pltpu.VMEM((own, 8, chunk), F32),
-                pltpu.VMEM((3, own, 8, chunk), F32),
-                pltpu.VMEM((own, feat, chunk), F32),
+                pltpu.VMEM((own, 8, chunk), F32),
                 pltpu.VMEM((T, chunk), F32),
                 pltpu.VMEM((2, chunk // 128, chunk, 128), BF16),
-                pltpu.VMEM((4, 8, 128), F32),
                 DMA((own + 1,)), DMA((2,)), DMA((2,)), DMA((2,)), DMA((2,)), DMA, DMA, DMA((3,)), DMA((3,)), DMA((3,)), DMA((3,)),
             ],
             compiler_params=pltpu.CompilerParams(collective_id=0, has_side_effects=True, vmem_limit_bytes=48 * 1024 * 1024),
         )
-        force, energy = call(pltpu.with_memory_space_constraint(pos_loc.reshape(own, chunk, feat), pltpu.HBM),
-                             pltpu.with_memory_space_constraint(chg_loc.reshape(rows // 128, 128), pltpu.HBM))
-        return force, energy[0, :1]
+        x_blocks = pos_loc.reshape(own, chunk, feat)
+        pulled, sums, parts = call(pltpu.with_memory_space_constraint(x_blocks, pltpu.HBM),
+                                   pltpu.with_memory_space_constraint(chg_loc.reshape(rows // 128, 128), pltpu.HBM))
+        force, energy = pl.pallas_call(
+            finish,
+            out_shape=[jax.ShapeDtypeStruct((own, chunk, feat), F32), jax.ShapeDtypeStruct((1,), F32)],
+            in_specs=[pl.BlockSpec(memory_space=pltpu.VMEM)] * 4,
+            out_specs=[pl.BlockSpec(memory_space=pltpu.HBM), pl.BlockSpec(memory_space=pltpu.SMEM)],
+            scratch_shapes=[pltpu.VMEM((own, chunk, feat), F32), DMA((own,))],
+            compiler_params=pltpu.CompilerParams(vmem_limit_bytes=8 * 1024 * 1024),
+        )(x_blocks, pulled, sums, parts)
+        return force.reshape(rows, feat), energy
 
     return jax.shard_map(device_body, mesh=mesh, in_specs=(P(("sys", "row"), None), P(("sys", "row"))), out_specs=(P(("sys", "row"), None), P("sys")), check_vma=False)

time: 29.7 us -> 29.4 us (0.990)
  local copies, waits for them, and re-layouts: 1.48 us -> 0.01 us
  Pallas kernels: 27.4 us -> 28.4 us
    pallas_call x1 -> x2, Pallas kernels: 27.4 us -> 28.4 us  [the longest x1 26.6 us: device_body(): call(pltpu.with_memory_space_constraint(x_blocks, pltpu.HBM), pltpu.with_...]
    unnamed x1 -> x2, local copies, waits for them, and re-layouts: 0.97 us -> 0.01 us
    slice x1 -> x0, local copies, waits for them, and re-layouts: 0.51 us -> none  [device_body(): return (force, energy[0, :1])]
where the time goes in v4:
time: 29.4 us; the launch traced here: 29.3 us
  Pallas kernels  28.4 us (97%)
  between operations  0.81 us (3%)
    pallas_call x1, Pallas kernels, device_body(): call(pltpu.with_memory_space_constraint(x_blocks, pltpu.HBM), pltpu.with_...  26.6 us
    pallas_call x1, Pallas kernels, device_body(): pl.pallas_call(finish, out_shape=[jax.ShapeDtypeStruct((own, chunk, feat)...  1.88 us

profile of v4, /device:TPU:0, one launch (start us, length us, event | category | flops | bytes accessed | tf_op | source)
XLA Modules:
  0.0 29.3 jit_solution(6433106952270219826)
XLA Ops:
  0.6 0.0 copy-start
  0.6 26.6 %shard_map.41 = (f32[4,128,512]{2,1,0:T(8,128)S(1)}, f32[3,4,8,512]{3,2,1,0:T(8,128)S(1)}, f32[4,8,128]{2,1,0:T(8,128)S(1)}) custom-call(bf16[4,512,128]{2,1,0:T(8,128)(2,1)} %bitcast.3, f32[16,128]{1,0:T(8,128)} %bitcast.5), custom_call_target="tpu_custom_call" | custom-call | tf_op jit(solution)/shard_map/pallas_call | solution.py:252
  27.2 0.0 copy-done
  27.2 1.9 %shard_map.42 = (f32[4,512,128]{2,1,0:T(8,128)}, f32[1]{0:T(128)}) custom-call(bf16[4,512,128]{2,1,0:T(8,128)(2,1)S(1)} %bitcast.4, f32[4,128,512]{2,1,0:T(8,128)S(1)} %get-tuple-element.7.ft, f32[3,4,8,512]{3,2,1,0:T(8,128)S(1)} %get-tuple-element.8.rs, f32[4,8,128]{2,1,0:T(8,128)S(1)} %get-tuple-element.9.ebuf), custom_call_target="tpu_custom_call" | custom-call | tf_op jit(solution)/shard_map/pallas_call | solution.py:254
Async XLA Ops:
  0.6 26.6 %copy-start = (bf16[2048,128]{1,0:T(8,128)(2,1)S(1)}, bf16[2048,128]{1,0:T(8,128)(2,1)}, u32[]{:S(2)}) copy-start(bf16[2048,128]{1,0:T(8,128)(2,1)} %param.2) | copy-start | bytes 1572868
